TPU v7x, 32 devices: a whole 2x2x4 slice. The times are simulated.
32 devices in a mesh: dp: 4 (over y, core), vocab: 8 (over z, x).
Axes of the slice: x: 2, y: 2, z: 4, core: 2. Of those that a mesh axis runs over, the one named last changes fastest.
Arguments:
- student_hidden: bfloat16 [512, 2048], P('dp', 'vocab'), may hold values from -210 to 210
- student_blocks: bfloat16 [8, 1024, 4864], P('vocab', 'dp'), may hold values from -0.375 to 0.375
- teacher_logits: bfloat16 [512, 19456], P('dp', 'vocab'), may hold values from -16 to 308
- token_ids: int32 [512], P('dp'), may hold values from 0 to 19455
- loss_mask: int32 [512], P('dp'), may hold values from 0 to 1, as said below
Outputs:
- hidden_grad: bfloat16 [512, 2048], P('dp', 'vocab')
- token_kl: float32 [512], P('dp')
- sampled_logprob: float32 [512], P('dp')
- loss: float32 [], replicated
Inputs may be any that keep to these rules, and one draw needn't show every extreme that they name: `loss_mask`: in each block of 128 tokens the mask is 0 on a leading run of at most 64 tokens and 1 on the rest.
All inputs are finite; a program needn't handle non-finite values.
Results may differ from a plain program's by a relative error of at most 0.0047.
Values may be sent and summed in bfloat16 or wider, within the bound.
No kernel may reach another device: no remote copies, remote signals or barrier semaphores. Data moves between devices by JAX's collectives and lax.ppermute only.
A program may use at most 64 MiB of HBM per device.

v0:
```python
import jax
import jax.numpy as jnp
from jax import lax
from jax.sharding import PartitionSpec as P

D = 2048
VT = 2432


def swapped(shard, axis, stride):
    return lax.ppermute(shard, axis, [(i, i ^ 1 << stride) for i in range(lax.axis_size(axis))])


def combined_all(part, axis, combine):
    gathered = jax.tree.map(lambda a: lax.all_gather(a, axis), part)

    def take(source):
        return jax.tree.map(lambda a: lax.dynamic_index_in_dim(a, source, 0, False), gathered)

    return lax.fori_loop(
        1, lax.axis_size(axis), lambda source, state: combine(state, take(source)), take(0)
    )


def pair_merge(left_pair, right_pair):
    left_max, left_total = left_pair
    right_max, right_total = right_pair
    top_value = jnp.maximum(left_max, right_max)
    merged_total = left_total * jnp.exp(left_max - top_value) + right_total * jnp.exp(
        right_max - top_value
    )
    return (top_value, merged_total)


def row_stats(values):
    row_max = jnp.max(values, axis=1)
    row_total = jnp.sum(jnp.exp(values - row_max[:, None]), axis=1)
    return (row_max, row_total)


def on_device(student_hidden, student_blocks, teacher_logits, token_ids, loss_mask):
    vocab_index = lax.axis_index("vocab")
    pair_side = vocab_index % 2
    mask_float = loss_mask.astype(jnp.float32)
    mask_total = lax.psum(jnp.sum(mask_float), "dp")
    gathered = lax.all_gather(student_hidden, "vocab", axis=1, tiled=True)
    piece = student_blocks[0]
    own_block = lax.dynamic_slice_in_dim(piece, pair_side * VT, VT, 1)
    far_block = lax.dynamic_slice_in_dim(piece, (1 - pair_side) * VT, VT, 1)
    received = swapped(far_block, "vocab", 0)
    stacked = jnp.where(
        pair_side == 0, jnp.stack([own_block, received]), jnp.stack([received, own_block])
    )
    weight = lax.all_gather(stacked, "dp", axis=1, tiled=True).reshape(D, VT)
    logits = jnp.dot(gathered, weight, preferred_element_type=jnp.float32)
    column_start = vocab_index * VT
    teacher_local = teacher_logits.astype(jnp.float32)
    teacher_full = teacher_logits.astype(jnp.float32)
    teacher_max = lax.pmax(jnp.max(teacher_full, axis=1), "vocab")
    teacher_total = lax.psum(jnp.sum(jnp.exp(teacher_full - teacher_max[:, None]), axis=1), "vocab")
    student_max, student_total = row_stats(logits)
    merged = combined_all((student_max, student_total), "vocab", pair_merge)
    stats = (teacher_max, teacher_total, merged[0], merged[1])
    teacher_logp = teacher_local - stats[0][:, None] - jnp.log(stats[1])[:, None]
    student_logp = logits - stats[2][:, None] - jnp.log(stats[3])[:, None]
    teacher_prob = jnp.exp(teacher_logp)
    kl_part = jnp.sum(teacher_prob * (teacher_logp - student_logp), axis=1)
    columns = lax.broadcasted_iota(jnp.int32, logits.shape, 1) + column_start
    sampled_part = jnp.sum(jnp.where(columns == token_ids[:, None], student_logp, 0.0), axis=1)
    token_kl, sampled = lax.psum((kl_part, sampled_part), "vocab")
    loss = lax.psum(jnp.sum(mask_float * token_kl), "dp") / mask_total
    factor = mask_float / mask_total
    dlogits = (factor[:, None] * (jnp.exp(student_logp) - teacher_prob)).astype(jnp.bfloat16)
    term = lax.dot_general(
        dlogits, weight, (((1,), (1,)), ((), ())), preferred_element_type=jnp.float32
    )
    hidden_grad = lax.psum_scatter(term, "vocab", scatter_dimension=1, tiled=True).astype(
        jnp.bfloat16
    )
    return (hidden_grad, token_kl, sampled, loss)


def solution(mesh):
    return jax.shard_map(
        on_device,
        mesh=mesh,
        in_specs=(P("dp", "vocab"), P("vocab", "dp", None), P("dp", "vocab"), P("dp"), P("dp")),
        out_specs=(P("dp", "vocab"), P("dp"), P("dp"), P()),
        check_vma=False,
    )
```

profile of v0, /device:TPU:0, one launch (start us, length us, event | category | flops | bytes accessed | tf_op | source)
XLA Modules:
  0.0 265.2 jit_solution(2844016320098941567)
XLA Ops:
  7.2 2.9 %constant_dynamic-slice_fusion.1 = (bf16[1,256,2432]{2,1,0:T(8,128)(2,1)S(1)}, bf16[256,2432]{1,0:T(8,128)(2,1)}) fusion(bf16[1,256,4864]{2,1,0:T(8,128)(2,1)} %param.8, s32[]{:T(128)S(6)} %select_n.41, s32[]{:T(128)S(6)} %select_n.42), kind=kLoop, calls=%fused_computation.33 | loop fusion | bytes 4980744 | tf_op jit(solution)/shard_map/dynamic_slice | solution.py:48
  10.1 3.0 %collective-permute-start = (bf16[256,2432]{1,0:T(8,128)(2,1)}, bf16[256,2432]{1,0:T(8,128)(2,1)S(1)}, u32[]{:S(2)}, u32[]{:S(2)}) collective-permute-start(bf16[256,2432]{1,0:T(8,128)(2,1)} %get-tuple-element.160), channel_id=1, source_target_pairs={{0,1},{1,0},{2,3},{3,2},{4,5},{5,4},{6,7},{7,6},{8,9},{9,8},{10,11... | collective-permute-start | bytes 3735560 | tf_op jit(solution)/shard_map/ppermute | solution.py:11
  13.1 27.6 %collective-permute-done = bf16[256,2432]{1,0:T(8,128)(2,1)S(1)} collective-permute-done((bf16[256,2432]{1,0:T(8,128)(2,1)}, bf16[256,2432]{1,0:T(8,128)(2,1)S(1)}, u32[]{:S(2)}, u32[]{:S(2)}) %collective-permute-start) | collective-permute-done | bytes 1245216 | tf_op jit(solution)/shard_map/ppermute | solution.py:11
  40.7 1.8 maximum_select_fusion
  42.6 1.0 copy-done
  43.6 0.3 copy.10
  43.9 0.2 reduce_max.24
  44.1 21.9 %pmax.7 = f32[128]{0:T(128)S(1)} all-reduce(bf16[128]{0:T(256)(128)(2,1)S(1)} %reduce_max.24), channel_id=1, replica_groups=mesh['dp'=4,'vocab'=8] {'vocab'}, use_global_device_ids=true, to_apply=%region_7.8 | all-reduce | flops 128 | bytes 768 | tf_op jit(solution)/shard_map/pmax | solution.py:59
  66.0 0.3 exponential_reduce_fusion
  66.3 17.1 %psum.36 = f32[128]{0:T(128)S(1)} all-reduce(f32[128]{0:T(128)S(1)} %exponential_reduce_fusion), channel_id=1, replica_groups=mesh['dp'=4,'vocab'=8] {'vocab'}, use_global_device_ids=true, to_apply=%region_9.10 | all-reduce | flops 128 | bytes 1024 | tf_op jit(solution)/shard_map/psum | solution.py:60
  83.5 31.2 %all_gather.19 = bf16[128,2048]{1,0:T(8,128)(2,1)S(1)} all-gather(bf16[128,256]{1,0:T(8,128)(2,1)S(1)} %copy-done.1), channel_id=1, replica_groups=mesh['dp'=4,'vocab'=8] {'vocab'}, dimensions={1}, use_global_device_ids=true | all-gather | bytes 589824 | tf_op jit(solution)/shard_map/all_gather | solution.py:46
  114.7 6.6 %fusion.17 = (f32[128]{0:T(128)S(1)}, f32[2432,128]{1,0:T(8,128)S(1)}) fusion(bf16[2048,2432]{1,0:T(8,128)(2,1)} %bitcast.46, bf16[128,2048]{1,0:T(8,128)(2,1)S(1)} %all_gather.19), kind=kOutput, calls=%fused_computation.36 | convolution fusion | flops 1275379584 | bytes 11731456 | tf_op jit(solution)/shard_map/dot_general | solution.py:55
  121.4 0.3 exponential_reduce_fusion.1
  121.7 18.5 %all-gather.3 = f32[8,1,128]{2,1,0:T(1,128)S(1)} all-gather(f32[1,1,128]{2,1,0:T(1,128)S(1)} %bitcast.52), channel_id=3, replica_groups=mesh['dp'=4,'vocab'=8] {'vocab'}, dimensions={0}, use_global_device_ids=true | all-gather | bytes 4608 | tf_op jit(solution)/shard_map/all_gather | solution.py:15
  140.2 16.3 %all-gather.2 = f32[8,1,128]{2,1,0:T(1,128)S(1)} all-gather(f32[1,1,128]{2,1,0:T(1,128)S(1)} %bitcast.51), channel_id=2, replica_groups=mesh['dp'=4,'vocab'=8] {'vocab'}, dimensions={0}, use_global_device_ids=true | all-gather | bytes 4608 | tf_op jit(solution)/shard_map/all_gather | solution.py:15
  156.5 0.3 while.17
  156.8 1.1 fusion.7
  157.9 19.7 %all-reduce = (f32[128]{0:T(128)S(1)}, f32[128]{0:T(128)}) all-reduce(f32[128]{0:T(128)S(1)} %get-tuple-element.140, f32[128]{0:T(128)S(1)} %get-tuple-element.139), channel_id=1, replica_groups=mesh['dp'=4,'vocab'=8] {'vocab'}, use_global_device_ids=true, to_apply=%region_12.13 | all-reduce | flops 256 | bytes 2048 | tf_op jit(solution)/shard_map/psum | solution.py:70
  177.6 0.6 multiply_reduce_fusion
  178.2 6.3 %all-reduce.1 = (f32[]{:T(128)}, f32[]{:T(128)}) all-reduce(f32[]{:T(128)} %get-tuple-element.142, f32[]{:T(128)} %get-tuple-element.141), channel_id=1, replica_groups=mesh['dp'=4,'vocab'=8] {'dp'}, use_global_device_ids=true, to_apply=%region_1.2 | all-reduce | flops 2 | bytes 16 | tf_op jit(solution)/shard_map/psum | solution.py:45
  184.4 0.6 convert_divide_fusion
  185.1 8.2 %fusion.10 = f32[128,2048]{1,0:T(8,128)} fusion(bf16[2048,2432]{1,0:T(8,128)(2,1)} %bitcast.47, bf16[128,2432]{0,1:T(8,128)(2,1)S(1)} %copy.10, f32[2432,128]{1,0:T(8,128)S(1)} %get-tuple-element.162, f32[128]{0:T(128)S(1)} %log.7, f32[128]{0:T(128)S(1)} %pmax.7, f32[128]{0:T(128)S(1)} %log.6, f32[128]{0:T(128)S(1)} %get-tuple-element.137, ...), kind=kOutput, calls=%fused_computation.23 | convolution fusion | flops 1277558784 | bytes 12880384 | tf_op jit(solution)/shard_map/dot_general | solution.py:74
  194.7 61.0 %reduce-scatter.2.cloned.1.call-done = f32[128,256]{1,0:T(8,128)} async-done(((f32[128,2048]{1,0:T(8,128)}), f32[128,256]{1,0:T(8,128)}) %reduce-scatter.2.cloned.1.call-update) | async-done | bytes 131088 | tf_op jit(solution)/shard_map/reduce_scatter | solution.py:77
  255.7 1.5 convert_element_type.16
  (26 shorter events, 0.3 us)
Async XLA Ops:
  7.2 107.5 %all-gather.6.cloned.1.call-start = ((), (), s32[]{:S(2)}) async-start(), calls=%async_computation.1 | async-start | bytes 12451840 | tf_op jit(solution)/shard_map/all_gather | solution.py:54
  10.1 30.5 %collective-permute-start = (bf16[256,2432]{1,0:T(8,128)(2,1)}, bf16[256,2432]{1,0:T(8,128)(2,1)S(1)}, u32[]{:S(2)}, u32[]{:S(2)}) collective-permute-start(bf16[256,2432]{1,0:T(8,128)(2,1)} %get-tuple-element.160), channel_id=1, source_target_pairs={{0,1},{1,0},{2,3},{3,2},{4,5},{5,4},{6,7},{7,6},{8,9},{9,8},{10,11... | collective-permute-start | bytes 3735560 | tf_op jit(solution)/shard_map/ppermute | solution.py:11
  42.5 1.1 copy-start
  42.5 213.1 %reduce-scatter.2.cloned.1.call-start = ((), (), s32[]{:S(2)}) async-start(), calls=%async_computation.2 | async-start | bytes 1179648 | tf_op jit(solution)/shard_map/reduce_scatter | solution.py:77
  43.6 39.9 %copy-start.1 = (bf16[128,256]{1,0:T(8,128)(2,1)S(1)}, bf16[128,256]{1,0:T(8,128)(2,1)}, u32[]{:S(2)}) copy-start(bf16[128,256]{1,0:T(8,128)(2,1)} %param.7) | copy-start | bytes 196612
  121.4 35.4 %copy-start.2 = (s32[128]{0:T(128)S(1)}, s32[128]{0:T(128)}, u32[]{:S(2)}) copy-start(s32[128]{0:T(128)} %param.10) | copy-start | bytes 1540
  121.7 55.9 %copy-start.3 = (s32[128]{0:T(128)S(1)}, s32[128]{0:T(128)}, u32[]{:S(2)}) copy-start(s32[128]{0:T(128)} %param.11) | copy-start | bytes 1540
  177.6 15.8 %copy-start.4 = (f32[128]{0:T(128)}, f32[128]{0:T(128)S(1)}, u32[]{:S(2)}) copy-start(f32[128]{0:T(128)S(1)} %get-tuple-element.153) | copy-start | bytes 1540
Sparse Core Ops, SparseCore 0:
  42.6 68.6 all-gather.5
  193.5 62.1 reduce-scatter.1
where the time goes:
time: 266 us; the launch traced here: 265 us
  blocking collectives  131 us (49%)
  waiting for transfers between devices  88.6 us (33%)
  between operations  16.6 us (6%)
  matrix products  14.9 us (6%)
  other arithmetic  6.81 us (3%)
  local copies, waits for them, and re-layouts  4.23 us (2%)
  starting transfers between devices  3.05 us (1%)
    reduce_scatter x1, waiting for transfers between devices, on_device(): lax.psum_scatter(term, 'vocab', scatter_dimension=1, tiled=True)  61 us
    all_gather x2, blocking collectives, combined_all(): gathered = jax.tree.map(lambda a: lax.all_gather(a, axis), part)  34.7 us
    all_gather x1, blocking collectives, on_device(): gathered = lax.all_gather(student_hidden, 'vocab', axis=1, tiled=True)  31.2 us
    ppermute x1, waiting for transfers between devices, swapped(): lax.ppermute(shard, axis, [(i, i ^ 1 << stride) for i in range(lax.axis_s...  27.6 us
    pmax x1, blocking collectives, on_device(): teacher_max = lax.pmax(jnp.max(teacher_full, axis=1), 'vocab')  21.9 us
    psum x1, blocking collectives, on_device(): token_kl, sampled = lax.psum((kl_part, sampled_part), 'vocab')  19.7 us
    psum x1, blocking collectives, on_device(): lax.psum(jnp.sum(jnp.exp(teacher_full - teacher_max[:, None]), axis=1), '...  17.1 us
    dot_general x1, matrix products, on_device(): lax.dot_general(dlogits, weight, (((1,), (1,)), ((), ())), preferred_elem...  8.22 us
  transfers between devices with their start and end apart: 3, of which 2 were waited for; matrix products, arithmetic and copies ran while one was open for 0% of the time, Pallas kernels for 0%

commit v1 on v0

--- a/solution.py
+++ b/solution.py
@@ -2,6 +2,7 @@
 import jax.numpy as jnp
 from jax import lax
 from jax.sharding import PartitionSpec as P
+from jax.lax import all_gather
 
 D = 2048
 VT = 2432
@@ -43,7 +44,7 @@
     pair_side = vocab_index % 2
     mask_float = loss_mask.astype(jnp.float32)
     mask_total = lax.psum(jnp.sum(mask_float), "dp")
-    gathered = lax.all_gather(student_hidden, "vocab", axis=1, tiled=True)
+    gathered = jnp.concatenate(all_gather(student_hidden, "vocab"), 1)
     piece = student_blocks[0]
     own_block = lax.dynamic_slice_in_dim(piece, pair_side * VT, VT, 1)
     far_block = lax.dynamic_slice_in_dim(piece, (1 - pair_side) * VT, VT, 1)

time: 266 us -> 266 us (level)
  no operation moved by 1% of the time
where the time goes in v1:
time: 266 us; the launch traced here: 265 us
  blocking collectives  131 us (49%)
  waiting for transfers between devices  88.6 us (33%)
  between operations  16.6 us (6%)
  matrix products  14.9 us (6%)
  other arithmetic  6.81 us (3%)
  local copies, waits for them, and re-layouts  4.26 us (2%)
  starting transfers between devices  3.05 us (1%)
    reduce_scatter x1, waiting for transfers between devices, on_device(): lax.psum_scatter(term, 'vocab', scatter_dimension=1, tiled=True)  61 us
    all_gather x2, blocking collectives, combined_all(): gathered = jax.tree.map(lambda a: lax.all_gather(a, axis), part)  34.7 us
    all_gather x1, blocking collectives, on_device(): gathered = jnp.concatenate(all_gather(student_hidden, 'vocab'), 1)  32 us
    ppermute x1, waiting for transfers between devices, swapped(): lax.ppermute(shard, axis, [(i, i ^ 1 << stride) for i in range(lax.axis_s...  27.6 us
    pmax x1, blocking collectives, on_device(): teacher_max = lax.pmax(jnp.max(teacher_full, axis=1), 'vocab')  21.2 us
    psum x1, blocking collectives, on_device(): token_kl, sampled = lax.psum((kl_part, sampled_part), 'vocab')  19.6 us
    psum x1, blocking collectives, on_device(): lax.psum(jnp.sum(jnp.exp(teacher_full - teacher_max[:, None]), axis=1), '...  17.1 us
    dot_general x1, matrix products, on_device(): lax.dot_general(dlogits, weight, (((1,), (1,)), ((), ())), preferred_elem...  8.22 us
  transfers between devices with their start and end apart: 3, of which 2 were waited for; matrix products, arithmetic and copies ran while one was open for 0% of the time, Pallas kernels for 0%

profile of v1, /device:TPU:0, one launch (start us, length us, event | category | flops | bytes accessed | tf_op | source)
XLA Modules:
  0.0 265.2 jit_solution(5867003953455832097)
XLA Ops:
  7.2 2.9 %constant_dynamic-slice_fusion.1 = (bf16[1,256,2432]{2,1,0:T(8,128)(2,1)S(1)}, bf16[256,2432]{1,0:T(8,128)(2,1)}) fusion(bf16[1,256,4864]{2,1,0:T(8,128)(2,1)} %param.8, s32[]{:T(128)S(6)} %select_n.41, s32[]{:T(128)S(6)} %select_n.42), kind=kLoop, calls=%fused_computation.33 | loop fusion | bytes 4980744 | tf_op jit(solution)/shard_map/dynamic_slice | solution.py:49
  10.1 3.0 %collective-permute-start = (bf16[256,2432]{1,0:T(8,128)(2,1)}, bf16[256,2432]{1,0:T(8,128)(2,1)S(1)}, u32[]{:S(2)}, u32[]{:S(2)}) collective-permute-start(bf16[256,2432]{1,0:T(8,128)(2,1)} %get-tuple-element.160), channel_id=1, source_target_pairs={{0,1},{1,0},{2,3},{3,2},{4,5},{5,4},{6,7},{7,6},{8,9},{9,8},{10,11... | collective-permute-start | bytes 3735560 | tf_op jit(solution)/shard_map/ppermute | solution.py:12
  13.1 27.6 %collective-permute-done = bf16[256,2432]{1,0:T(8,128)(2,1)S(1)} collective-permute-done((bf16[256,2432]{1,0:T(8,128)(2,1)}, bf16[256,2432]{1,0:T(8,128)(2,1)S(1)}, u32[]{:S(2)}, u32[]{:S(2)}) %collective-permute-start) | collective-permute-done | bytes 1245216 | tf_op jit(solution)/shard_map/ppermute | solution.py:12
  40.7 1.8 maximum_select_fusion
  42.6 0.8 copy-done.1
  43.3 32.0 %all-gather = bf16[1024,256]{1,0:T(8,128)(2,1)S(1)} all-gather(bf16[128,256]{1,0:T(8,128)(2,1)S(1)} %copy-done.1), channel_id=2, replica_groups=mesh['dp'=4,'vocab'=8] {'vocab'}, dimensions={0}, use_global_device_ids=true | all-gather | bytes 589824 | tf_op jit(solution)/shard_map/all_gather | solution.py:47
  75.3 0.3 copy.13
  75.6 0.3 copy.14
  76.1 21.2 %pmax.7 = f32[128]{0:T(128)S(1)} all-reduce(bf16[128]{0:T(256)(128)(2,1)S(1)} %reduce_max.24), channel_id=1, replica_groups=mesh['dp'=4,'vocab'=8] {'vocab'}, use_global_device_ids=true, to_apply=%region_7.8 | all-reduce | flops 128 | bytes 768 | tf_op jit(solution)/shard_map/pmax | solution.py:60
  97.3 0.3 exponential_reduce_fusion
  97.6 17.1 %psum.36 = f32[128]{0:T(128)S(1)} all-reduce(f32[128]{0:T(128)S(1)} %exponential_reduce_fusion), channel_id=1, replica_groups=mesh['dp'=4,'vocab'=8] {'vocab'}, use_global_device_ids=true, to_apply=%region_9.10 | all-reduce | flops 128 | bytes 1024 | tf_op jit(solution)/shard_map/psum | solution.py:61
  114.8 6.6 %fusion.17 = (f32[128]{0:T(128)S(1)}, f32[2432,128]{1,0:T(8,128)S(1)}) fusion(bf16[2048,2432]{1,0:T(8,128)(2,1)} %bitcast.50, bf16[128,2048]{0,1:T(8,128)(2,1)S(1)} %bitcast.54), kind=kOutput, calls=%fused_computation.36 | convolution fusion | flops 1275379584 | bytes 11731456 | tf_op jit(solution)/shard_map/dot_general | solution.py:56
  121.4 0.3 exponential_reduce_fusion.1
  121.8 18.4 %all-gather.4 = f32[8,1,128]{2,1,0:T(1,128)S(1)} all-gather(f32[1,1,128]{2,1,0:T(1,128)S(1)} %bitcast.58), channel_id=4, replica_groups=mesh['dp'=4,'vocab'=8] {'vocab'}, dimensions={0}, use_global_device_ids=true | all-gather | bytes 4608 | tf_op jit(solution)/shard_map/all_gather | solution.py:16
  140.2 16.3 %all-gather.3 = f32[8,1,128]{2,1,0:T(1,128)S(1)} all-gather(f32[1,1,128]{2,1,0:T(1,128)S(1)} %bitcast.57), channel_id=3, replica_groups=mesh['dp'=4,'vocab'=8] {'vocab'}, dimensions={0}, use_global_device_ids=true | all-gather | bytes 4608 | tf_op jit(solution)/shard_map/all_gather | solution.py:16
  156.5 0.3 while.17
  156.8 1.1 fusion.7
  157.9 19.6 %all-reduce = (f32[128]{0:T(128)S(1)}, f32[128]{0:T(128)}) all-reduce(f32[128]{0:T(128)S(1)} %get-tuple-element.140, f32[128]{0:T(128)S(1)} %get-tuple-element.139), channel_id=1, replica_groups=mesh['dp'=4,'vocab'=8] {'vocab'}, use_global_device_ids=true, to_apply=%region_12.13 | all-reduce | flops 256 | bytes 2048 | tf_op jit(solution)/shard_map/psum | solution.py:71
  177.6 0.6 multiply_reduce_fusion
  178.2 6.3 %all-reduce.1 = (f32[]{:T(128)}, f32[]{:T(128)}) all-reduce(f32[]{:T(128)} %get-tuple-element.142, f32[]{:T(128)} %get-tuple-element.141), channel_id=1, replica_groups=mesh['dp'=4,'vocab'=8] {'dp'}, use_global_device_ids=true, to_apply=%region_1.2 | all-reduce | flops 2 | bytes 16 | tf_op jit(solution)/shard_map/psum | solution.py:46
  184.4 0.6 convert_divide_fusion
  185.1 8.2 %fusion.10 = f32[128,2048]{1,0:T(8,128)} fusion(bf16[2048,2432]{1,0:T(8,128)(2,1)} %bitcast.51, bf16[128,2432]{0,1:T(8,128)(2,1)S(1)} %copy.14, f32[2432,128]{1,0:T(8,128)S(1)} %get-tuple-element.162, f32[128]{0:T(128)S(1)} %log.7, f32[128]{0:T(128)S(1)} %pmax.7, f32[128]{0:T(128)S(1)} %log.6, f32[128]{0:T(128)S(1)} %get-tuple-element.137, ...), kind=kOutput, calls=%fused_computation.23 | convolution fusion | flops 1277558784 | bytes 12880384 | tf_op jit(solution)/shard_map/dot_general | solution.py:75
  194.7 61.0 %reduce-scatter.2.cloned.1.call-done = f32[128,256]{1,0:T(8,128)} async-done(((f32[128,2048]{1,0:T(8,128)}), f32[128,256]{1,0:T(8,128)}) %reduce-scatter.2.cloned.1.call-update) | async-done | bytes 131088 | tf_op jit(solution)/shard_map/reduce_scatter | solution.py:78
  255.7 1.5 convert_element_type.16
  (27 shorter events, 0.5 us)
Async XLA Ops:
  7.2 107.6 %all-gather.7.cloned.1.call-start = ((), (), s32[]{:S(2)}) async-start(), calls=%async_computation.1 | async-start | bytes 12451840 | tf_op jit(solution)/shard_map/all_gather | solution.py:55
  10.1 30.5 %collective-permute-start = (bf16[256,2432]{1,0:T(8,128)(2,1)}, bf16[256,2432]{1,0:T(8,128)(2,1)S(1)}, u32[]{:S(2)}, u32[]{:S(2)}) collective-permute-start(bf16[256,2432]{1,0:T(8,128)(2,1)} %get-tuple-element.160), channel_id=1, source_target_pairs={{0,1},{1,0},{2,3},{3,2},{4,5},{5,4},{6,7},{7,6},{8,9},{9,8},{10,11... | collective-permute-start | bytes 3735560 | tf_op jit(solution)/shard_map/ppermute | solution.py:12
  42.5 0.8 copy-start.1
  42.5 33.1 %copy-start = (bf16[128,2432]{1,0:T(8,128)(2,1)S(1)}, bf16[128,2432]{1,0:T(8,128)(2,1)}, u32[]{:S(2)}) copy-start(bf16[128,2432]{1,0:T(8,128)(2,1)} %param.9) | copy-start | bytes 1867780
  42.5 213.2 %reduce-scatter.2.cloned.1.call-start = ((), (), s32[]{:S(2)}) async-start(), calls=%async_computation.2 | async-start | bytes 1179648 | tf_op jit(solution)/shard_map/reduce_scatter | solution.py:78
  121.4 35.3 %copy-start.2 = (s32[128]{0:T(128)S(1)}, s32[128]{0:T(128)}, u32[]{:S(2)}) copy-start(s32[128]{0:T(128)} %param.10) | copy-start | bytes 1540
  121.8 55.8 %copy-start.3 = (s32[128]{0:T(128)S(1)}, s32[128]{0:T(128)}, u32[]{:S(2)}) copy-start(s32[128]{0:T(128)} %param.11) | copy-start | bytes 1540
  177.6 15.8 %copy-start.4 = (f32[128]{0:T(128)}, f32[128]{0:T(128)S(1)}, u32[]{:S(2)}) copy-start(f32[128]{0:T(128)S(1)} %get-tuple-element.153) | copy-start | bytes 1540
Sparse Core Ops, SparseCore 0:
  42.6 68.6 all-gather.6
  193.5 62.1 reduce-scatter.1
